TPU v7x, 32 devices: a whole 2x2x4 slice. The times are simulated.
32 devices in a mesh: group: 8 (over z, x), peer: 4 (over y, core).
Axes of the slice: x: 2, y: 2, z: 4, core: 2. Of those that a mesh axis runs over, the one named last changes fastest.
Arguments:
- features: bfloat16 [12288, 1024], P(('group', 'peer')), may hold values from -6 to 6
- task_mask: int32 [12288], P(('group', 'peer')), may hold values from 0 to 65535, as said below
- tower_in: bfloat16 [16, 2048, 1024], P('peer', 'group'), may hold values from -0.1875 to 0.1875
- tower_bias: bfloat16 [16, 2048], P('peer', 'group'), may hold values from -5 to 5
- tower_head: bfloat16 [16, 2048], P('peer', 'group'), may hold values from -0.125 to 0.125
- head_bias: float32 [16], P('peer'), may hold values from -4 to 4
Outputs:
- predictions: float32 [12288, 16], P(('group', 'peer'))
Inputs may be any that keep to these rules, and one draw needn't show every extreme that they name: `task_mask`: only bits 0 to 15 are used. Among the 384 samples of one device (aligned blocks of 384), at most 176 have any one bit set; in every run of 4 blocks that one group holds, some task's bit is set exactly 176 times in each block.
All inputs are finite; a program needn't handle non-finite values.
Results may differ from a plain program's by a relative error of at most 0.0003.
Values may be sent and summed in bfloat16 or wider, within the bound.
A program may use at most 128 MiB of HBM per device.

v0:
```python
import jax
import jax.numpy as jnp
from jax import lax
from jax.sharding import PartitionSpec as P

CAP = 176


def shards(features, task_mask, tower_in, tower_bias, tower_head, head_bias):
    peers = lax.axis_size("peer")
    local_tasks = tower_in.shape[0]
    all_tasks = local_tasks * peers
    task_ids = jnp.arange(all_tasks, dtype=jnp.int32)
    slot_indices = jnp.arange(CAP, dtype=jnp.int32)
    task_bits = task_mask[:, None] >> task_ids[None, :] & 1
    inclusive = jnp.cumsum(task_bits, axis=0)
    slot_rank = inclusive - task_bits
    task_selector = (slot_rank.T[:, None, :] == slot_indices[None, :, None]) & (
        task_bits.T[:, None, :] == 1
    )
    outgoing = jnp.einsum(
        "yra,az->yrz",
        task_selector.astype(jnp.bfloat16),
        features,
        preferred_element_type=jnp.float32,
    ).astype(jnp.bfloat16)
    outgoing = outgoing.reshape(peers, local_tasks, CAP, features.shape[1])
    arrived = lax.all_to_all(outgoing, "peer", split_axis=0, concat_axis=0, tiled=True)
    weight = lax.all_gather(tower_in, "group", axis=1, tiled=True)
    hidden_unit_bias = lax.all_gather(tower_bias, "group", axis=1, tiled=True)
    head_row = lax.all_gather(tower_head, "group", axis=1, tiled=True)
    preact = jnp.einsum("sjcd,jhd->sjch", arrived, weight, preferred_element_type=jnp.float32)
    hidden = jnp.maximum(preact + hidden_unit_bias.astype(jnp.float32)[None, :, None, :], 0.0)
    logits = jnp.einsum(
        "sjch,jh->sjc", hidden, head_row.astype(jnp.float32), precision=lax.Precision.HIGHEST
    )
    logits = logits + head_bias[None, :, None]
    returned_output = lax.all_to_all(
        logits, "peer", split_axis=0, concat_axis=0, tiled=True
    ).reshape(all_tasks, CAP)
    task_selector = (slot_rank.T[:, None, :] == slot_indices[None, :, None]) & (
        task_bits.T[:, None, :] == 1
    )
    return jnp.einsum(
        "ivf,iv->fi",
        task_selector.astype(jnp.float32),
        returned_output,
        precision=lax.Precision.HIGHEST,
    )


def solution(mesh):
    placed = (
        P(("group", "peer"), None),
        P(("group", "peer")),
        P("peer", "group", None),
        P("peer", "group"),
        P("peer", "group"),
        P("peer"),
    )
    return jax.shard_map(
        shards, mesh=mesh, in_specs=placed, out_specs=P(("group", "peer"), None), check_vma=False
    )
```

profile of v0, /device:TPU:0, one launch (start us, length us, event | category | flops | bytes accessed | tf_op | source)
XLA Modules:
  0.0 291.0 jit_solution(16052179998820379908)
XLA Ops:
  6.5 0.0 copy-start
  6.5 0.0 all-gather.2.cloned.1.call-start
  6.5 0.7 all-gather.2.cloned.1.call-update
  7.3 0.7 shift-right-arithmetic_and_fusion.1
  7.9 0.9 reduce-window.6
  8.8 0.2 slice_reduce_fusion
  9.1 0.7 fusion.23
  9.8 0.8 bitcast_subtract_fusion
  10.5 0.0 copy-done
  10.5 4.9 %fusion.14 = bf16[16,176,1024]{2,1,0:T(8,128)(2,1)} fusion(s32[16,384]{1,0:T(8,128)S(1)} %bitcast_subtract_fusion, pred[16,384]{1,0:T(8,128)(4,1)S(1)} %fusion.23, bf16[384,1024]{1,0:T(8,128)(2,1)S(1)} %copy-done), kind=kOutput, calls=%fused_computation.13 | convolution fusion | flops 2219638784 | bytes 6584320 | tf_op jit(solution)/shard_map/yra,az->yrz/dot_general | solution.py:21
  15.4 0.0 copy-start.1
  15.4 0.0 copy-start.2
  15.4 5.3 %all-to-all-start = ((bf16[4,4,176,1024]{3,2,1,0:T(8,128)(2,1)}), bf16[4,4,176,1024]{3,2,1,0:T(8,128)(2,1)}, u32[]{:S(2)}, u32[]{:S(2)}) async-start(bf16[4,4,176,1024]{3,2,1,0:T(8,128)(2,1)} %bitcast.32), calls=%async_computation | async-start | bytes 11534336 | tf_op jit(solution)/shard_map/all_to_all | solution.py:28
  20.7 0.0 copy-done.1
  20.7 29.4 %all_gather.10 = bf16[4,2048]{1,0:T(4,128)(2,1)S(1)} all-gather(bf16[4,256]{1,0:T(4,128)(2,1)S(1)} %copy-done.1), channel_id=1, replica_groups=mesh['group'=8,'peer'=4] {'group'}, dimensions={1}, use_global_device_ids=true | all-gather | bytes 18432 | tf_op jit(solution)/shard_map/all_gather | solution.py:30
  50.2 0.0 copy-done.2
  50.2 27.3 %all_gather.11 = bf16[4,2048]{1,0:T(4,128)(2,1)S(1)} all-gather(bf16[4,256]{1,0:T(4,128)(2,1)S(1)} %copy-done.2), channel_id=1, replica_groups=mesh['group'=8,'peer'=4] {'group'}, dimensions={1}, use_global_device_ids=true | all-gather | bytes 18432 | tf_op jit(solution)/shard_map/all_gather | solution.py:31
  77.5 9.2 %all-to-all-done = bf16[4,4,176,1024]{3,2,1,0:T(8,128)(2,1)} async-done(((bf16[4,4,176,1024]{3,2,1,0:T(8,128)(2,1)}), bf16[4,4,176,1024]{3,2,1,0:T(8,128)(2,1)}, u32[]{:S(2)}, u32[]{:S(2)}) %all-to-all-start) | async-done | bytes 5767200 | tf_op jit(solution)/shard_map/all_to_all | solution.py:28
  86.7 153.3 %all-gather.2.cloned.1.call-done = bf16[4,2048,1024]{2,1,0:T(8,128)(2,1)} async-done(((bf16[4,256,1024]{2,1,0:T(8,128)(2,1)}), bf16[4,2048,1024]{2,1,0:T(8,128)(2,1)}) %all-gather.2.cloned.1.call-update) | async-done | bytes 16777232 | tf_op jit(solution)/shard_map/all_gather | solution.py:29
  240.0 20.6 %fusion.4 = f32[4,4,176,2048]{3,2,1,0:T(8,128)} fusion(bf16[4,2048,1024]{2,1,0:T(8,128)(2,1)} %all-gather.2.cloned.1.call-done, bf16[4,4,176,1024]{3,2,1,0:T(8,128)(2,1)} %all-to-all-done), kind=kOutput, calls=%fused_computation.4 | convolution fusion | flops 11811160064 | bytes 45613056 | tf_op jit(solution)/shard_map/sjcd,jhd->sjch/dot_general | solution.py:32
  260.6 0.0 copy-start.3
  260.6 14.7 %fusion = f32[4,1,4,176]{3,1,2,0:T(1,128)S(1)} fusion(f32[4,4,176,2048]{3,2,1,0:T(8,128)} %fusion.4, f32[4,2048]{1,0:T(4,128)S(1)} %convert_element_type.10, bf16[4,2048,1,1]{1,0,2,3:T(4,128)(2,1)S(1)} %bitcast.33), kind=kOutput, calls=%fused_computation | convolution fusion | flops 80740352 | bytes 23129088 | tf_op jit(solution)/shard_map/sjch,jh->sjc/dot_general | solution.py:34
  275.3 0.0 copy-done.3
  275.3 0.1 fusion.24
  275.4 6.4 %all_to_all.10 = f32[4,4,176]{2,1,0:T(4,128)S(1)} all-to-all(f32[4,4,176]{2,1,0:T(4,128)S(1)} %fusion.24), channel_id=1, replica_groups=mesh['group'=8,'peer'=4] {'peer'}, dimensions={0} | all-to-all | bytes 22528 | tf_op jit(solution)/shard_map/all_to_all | solution.py:38
  281.8 1.8 fusion.10
  283.6 0.6 copy.22
  (3 shorter events, 0.1 us)
Async XLA Ops:
  6.5 4.0 %copy-start = (bf16[384,1024]{1,0:T(8,128)(2,1)S(1)}, bf16[384,1024]{1,0:T(8,128)(2,1)}, u32[]{:S(2)}) copy-start(bf16[384,1024]{1,0:T(8,128)(2,1)} %param.6) | copy-start | bytes 2359300
  6.5 233.5 %all-gather.2.cloned.1.call-start = ((), (), s32[]{:S(2)}) async-start(), calls=%async_computation.2 | async-start | bytes 18874368 | tf_op jit(solution)/shard_map/all_gather | solution.py:29
  15.4 5.3 %copy-start.1 = (bf16[4,256]{1,0:T(4,128)(2,1)S(1)}, bf16[4,256]{1,0:T(4,128)(2,1)}, u32[]{:S(2)}) copy-start(bf16[4,256]{1,0:T(4,128)(2,1)} %param.9) | copy-start | bytes 6148
  15.4 34.7 %copy-start.2 = (bf16[4,256]{1,0:T(4,128)(2,1)S(1)}, bf16[4,256]{1,0:T(4,128)(2,1)}, u32[]{:S(2)}) copy-start(bf16[4,256]{1,0:T(4,128)(2,1)} %param.10) | copy-start | bytes 6148
  15.4 71.2 %all-to-all-start = ((bf16[4,4,176,1024]{3,2,1,0:T(8,128)(2,1)}), bf16[4,4,176,1024]{3,2,1,0:T(8,128)(2,1)}, u32[]{:S(2)}, u32[]{:S(2)}) async-start(bf16[4,4,176,1024]{3,2,1,0:T(8,128)(2,1)} %bitcast.32), calls=%async_computation | async-start | bytes 11534336 | tf_op jit(solution)/shard_map/all_to_all | solution.py:28
  260.6 14.7 %copy-start.3 = (f32[4]{0:T(128)S(1)}, f32[4]{0:T(128)}, u32[]{:S(2)}) copy-start(f32[4]{0:T(128)} %param.11) | copy-start | bytes 52
Sparse Core Ops, SparseCore 0:
  9.5 230.4 all-gather.1
where the time goes:
time: 291 us
  waiting for transfers between devices  163 us (56%)
  blocking collectives  63.1 us (22%)
  matrix products  42 us (14%)
  between operations  13.4 us (5%)
  starting transfers between devices  5.26 us (2%)
  other arithmetic  3.12 us (1%)
    all_gather x1, waiting for transfers between devices, shards(): weight = lax.all_gather(tower_in, 'group', axis=1, tiled=True)  153 us
    all_gather x1, blocking collectives, shards(): hidden_unit_bias = lax.all_gather(tower_bias, 'group', axis=1, tiled=True)  29.4 us
    all_gather x1, blocking collectives, shards(): head_row = lax.all_gather(tower_head, 'group', axis=1, tiled=True)  27.3 us
    dot_general x1, matrix products, shards(): jnp.einsum('sjcd,jhd->sjch', arrived, weight, preferred_element_type=jnp....  20.6 us
    dot_general x1, matrix products, shards(): jnp.einsum('sjch,jh->sjc', hidden, head_row.astype(jnp.float32), precisio...  14.7 us
    all_to_all x1, waiting for transfers between devices, shards(): lax.all_to_all(outgoing, 'peer', split_axis=0, concat_axis=0, tiled=True)  9.23 us
    all_to_all x1, blocking collectives, shards(): lax.all_to_all(logits, 'peer', split_axis=0, concat_axis=0, tiled=True)  6.38 us
  transfers between devices with their start and end apart: 2, of which 2 were waited for; matrix products, arithmetic and copies ran while one was open for 3% of the time, Pallas kernels for 0%

commit v1 on v0

--- a/solution.py
+++ b/solution.py
@@ -26,7 +26,7 @@
     ).astype(jnp.bfloat16)
     outgoing = outgoing.reshape(peers, local_tasks, CAP, features.shape[1])
     arrived = lax.all_to_all(outgoing, "peer", split_axis=0, concat_axis=0, tiled=True)
-    weight = lax.all_gather(tower_in, "group", axis=1, tiled=True)
+    weight = jnp.concatenate(lax.all_gather(tower_in, "group"), axis=1)
     hidden_unit_bias = lax.all_gather(tower_bias, "group", axis=1, tiled=True)
     head_row = lax.all_gather(tower_head, "group", axis=1, tiled=True)
     preact = jnp.einsum("sjcd,jhd->sjch", arrived, weight, preferred_element_type=jnp.float32)

time: 291 us -> 305 us (1.048)
  local copies, waits for them, and re-layouts: 0.88 us -> 14.7 us
    reshape x0 -> x1, local copies, waits for them, and re-layouts: none -> 13.9 us  [shards(): weight = jnp.concatenate(lax.all_gather(tower_in, 'group'), axis=1)]
    all_to_all x1, waiting for transfers between devices: 9.23 us -> 0.01 us  [shards(): lax.all_to_all(outgoing, 'peer', split_axis=0, concat_axis=0, tiled=True)]
    all_gather x1, waiting for transfers between devices: 153 us -> 161 us  [shards(): weight = jnp.concatenate(lax.all_gather(tower_in, 'group'), axis=1)]
  transfers between devices with their start and end apart: 2 -> 2, of which waited for: 2 -> 1; matrix products, arithmetic and copies ran while one was open for 3% -> 7% of each run, Pallas kernels for 0% -> 0%
where the time goes in v1:
time: 305 us
  waiting for transfers between devices  162 us (53%)
  blocking collectives  64.9 us (21%)
  matrix products  42 us (14%)
  local copies, waits for them, and re-layouts  14.7 us (5%)
  between operations  13.4 us (4%)
  starting transfers between devices  5.28 us (2%)
  other arithmetic  3.12 us (1%)
    all_gather x1, waiting for transfers between devices, shards(): weight = jnp.concatenate(lax.all_gather(tower_in, 'group'), axis=1)  161 us
    all_gather x1, blocking collectives, shards(): hidden_unit_bias = lax.all_gather(tower_bias, 'group', axis=1, tiled=True)  31.2 us
    all_gather x1, blocking collectives, shards(): head_row = lax.all_gather(tower_head, 'group', axis=1, tiled=True)  27.3 us
    dot_general x1, matrix products, shards(): jnp.einsum('sjcd,jhd->sjch', arrived, weight, preferred_element_type=jnp....  20.6 us
    dot_general x1, matrix products, shards(): jnp.einsum('sjch,jh->sjc', hidden, head_row.astype(jnp.float32), precisio...  14.8 us
    reshape x1, local copies, waits for them, and re-layouts, shards(): weight = jnp.concatenate(lax.all_gather(tower_in, 'group'), axis=1)  13.9 us
    all_to_all x1, blocking collectives, shards(): lax.all_to_all(logits, 'peer', split_axis=0, concat_axis=0, tiled=True)  6.39 us
  transfers between devices with their start and end apart: 2, of which 1 were waited for; matrix products, arithmetic and copies ran while one was open for 7% of the time, Pallas kernels for 0%

profile of v1, /device:TPU:0, one launch (start us, length us, event | category | flops | bytes accessed | tf_op | source)
XLA Modules:
  0.0 305.0 jit_solution(15945945430129793686)
XLA Ops:
  6.5 0.0 copy-start
  6.5 0.0 all-gather.3.cloned.1.call-start
  6.5 0.7 all-gather.3.cloned.1.call-update
  7.3 0.7 shift-right-arithmetic_and_fusion.1
  7.9 0.9 reduce-window.6
  8.8 0.2 slice_reduce_fusion
  9.1 0.7 fusion.22
  9.8 0.8 bitcast_subtract_fusion
  10.5 0.0 copy-done
  10.5 4.9 %fusion.13 = bf16[16,176,1024]{2,1,0:T(8,128)(2,1)} fusion(s32[16,384]{1,0:T(8,128)S(1)} %bitcast_subtract_fusion, pred[16,384]{1,0:T(8,128)(4,1)S(1)} %fusion.22, bf16[384,1024]{1,0:T(8,128)(2,1)S(1)} %copy-done), kind=kOutput, calls=%fused_computation.12 | convolution fusion | flops 2219638784 | bytes 6584320 | tf_op jit(solution)/shard_map/yra,az->yrz/dot_general | solution.py:21
  15.4 0.0 copy-start.2
  15.4 0.0 copy-start.3
  15.4 5.3 %all-to-all-start = ((bf16[4,4,176,1024]{3,2,1,0:T(8,128)(2,1)}), bf16[4,4,176,1024]{3,2,1,0:T(8,128)(2,1)}, u32[]{:S(2)}, u32[]{:S(2)}) async-start(bf16[4,4,176,1024]{3,2,1,0:T(8,128)(2,1)} %bitcast.38), calls=%async_computation | async-start | bytes 11534336 | tf_op jit(solution)/shard_map/all_to_all | solution.py:28
  20.7 0.0 copy-done.2
  20.7 31.2 %all_gather.14 = bf16[4,2048]{1,0:T(4,128)(2,1)S(1)} all-gather(bf16[4,256]{1,0:T(4,128)(2,1)S(1)} %copy-done.2), channel_id=1, replica_groups=mesh['group'=8,'peer'=4] {'group'}, dimensions={1}, use_global_device_ids=true | all-gather | bytes 18432 | tf_op jit(solution)/shard_map/all_gather | solution.py:30
  51.9 0.0 copy-done.3
  51.9 27.3 %all_gather.15 = bf16[4,2048]{1,0:T(4,128)(2,1)S(1)} all-gather(bf16[4,256]{1,0:T(4,128)(2,1)S(1)} %copy-done.3), channel_id=1, replica_groups=mesh['group'=8,'peer'=4] {'group'}, dimensions={1}, use_global_device_ids=true | all-gather | bytes 18432 | tf_op jit(solution)/shard_map/all_gather | solution.py:31
  79.2 160.8 %all-gather.3.cloned.1.call-done = bf16[32,256,1024]{2,1,0:T(8,128)(2,1)} async-done(((bf16[4,256,1024]{2,1,0:T(8,128)(2,1)}), bf16[32,256,1024]{2,1,0:T(8,128)(2,1)}) %all-gather.3.cloned.1.call-update) | async-done | bytes 16777232 | tf_op jit(solution)/shard_map/all_gather | solution.py:29
  240.0 13.9 %copy.12 = bf16[4,8,256,1024]{3,2,1,0:T(8,128)(2,1)} copy(bf16[4,8,256,1024]{3,2,0,1:T(8,128)(2,1)} %bitcast.36) | data formatting | bytes 33554432 | tf_op jit(solution)/shard_map/reshape | solution.py:29
  253.9 0.0 all-to-all-done
  253.9 20.6 %fusion.6 = f32[4,4,176,2048]{3,2,1,0:T(8,128)} fusion(bf16[4,2048,1024,1]{2,1,3,0:T(8,128)(2,1)} %bitcast.37, bf16[4,4,176,1024]{3,2,1,0:T(8,128)(2,1)} %all-to-all-done), kind=kOutput, calls=%fused_computation.6 | convolution fusion | flops 11811160064 | bytes 45613056 | tf_op jit(solution)/shard_map/sjcd,jhd->sjch/dot_general | solution.py:32
  274.5 0.0 copy-start.4
  274.5 0.0 copy-start.1
  274.5 14.8 %fusion = f32[4,1,4,176]{3,1,2,0:T(1,128)S(1)} fusion(f32[4,4,176,2048]{3,2,1,0:T(8,128)} %fusion.6, f32[4,2048]{1,0:T(4,128)S(1)} %convert_element_type.10, bf16[4,2048,1,1]{1,0,2,3:T(4,128)(2,1)S(1)} %bitcast.39), kind=kOutput, calls=%fused_computation | convolution fusion | flops 80740352 | bytes 23129088 | tf_op jit(solution)/shard_map/sjch,jh->sjc/dot_general | solution.py:34
  289.3 0.0 copy-done.4
  289.3 0.1 fusion.23
  289.3 6.4 %all_to_all.10 = f32[4,4,176]{2,1,0:T(4,128)S(1)} all-to-all(f32[4,4,176]{2,1,0:T(4,128)S(1)} %fusion.23), channel_id=1, replica_groups=mesh['group'=8,'peer'=4] {'peer'}, dimensions={0} | all-to-all | bytes 22528 | tf_op jit(solution)/shard_map/all_to_all | solution.py:38
  295.8 1.8 fusion.9
  297.6 0.6 copy.27
  298.2 0.0 copy-done.1
  (3 shorter events, 0.1 us)
Async XLA Ops:
  6.5 4.0 %copy-start = (bf16[384,1024]{1,0:T(8,128)(2,1)S(1)}, bf16[384,1024]{1,0:T(8,128)(2,1)}, u32[]{:S(2)}) copy-start(bf16[384,1024]{1,0:T(8,128)(2,1)} %param.6) | copy-start | bytes 2359300
  6.5 233.5 %all-gather.3.cloned.1.call-start = ((), (), s32[]{:S(2)}) async-start(), calls=%async_computation.2 | async-start | bytes 18874368 | tf_op jit(solution)/shard_map/all_gather | solution.py:29
  15.4 5.3 %copy-start.2 = (bf16[4,256]{1,0:T(4,128)(2,1)S(1)}, bf16[4,256]{1,0:T(4,128)(2,1)}, u32[]{:S(2)}) copy-start(bf16[4,256]{1,0:T(4,128)(2,1)} %param.9) | copy-start | bytes 6148
  15.4 36.5 %copy-start.3 = (bf16[4,256]{1,0:T(4,128)(2,1)S(1)}, bf16[4,256]{1,0:T(4,128)(2,1)}, u32[]{:S(2)}) copy-start(bf16[4,256]{1,0:T(4,128)(2,1)} %param.10) | copy-start | bytes 6148
  15.4 238.5 %all-to-all-start = ((bf16[4,4,176,1024]{3,2,1,0:T(8,128)(2,1)}), bf16[4,4,176,1024]{3,2,1,0:T(8,128)(2,1)}, u32[]{:S(2)}, u32[]{:S(2)}) async-start(bf16[4,4,176,1024]{3,2,1,0:T(8,128)(2,1)} %bitcast.38), calls=%async_computation | async-start | bytes 11534336 | tf_op jit(solution)/shard_map/all_to_all | solution.py:28
  274.5 14.8 %copy-start.4 = (f32[4]{0:T(128)S(1)}, f32[4]{0:T(128)}, u32[]{:S(2)}) copy-start(f32[4]{0:T(128)} %param.11) | copy-start | bytes 52
  274.5 23.7 %copy-start.1 = (bf16[384,1024]{1,0:T(8,128)(2,1)S(1)}, bf16[384,1024]{1,0:T(8,128)(2,1)}, u32[]{:S(2)}) copy-start(bf16[384,1024]{1,0:T(8,128)(2,1)} %param.6) | copy-start | bytes 2359300
Sparse Core Ops, SparseCore 0:
  9.5 230.5 all-gather.2
